TPU v7x, 32 devices: a whole 2x2x4 slice. The times are simulated.
32 devices in a mesh: gx: 8 (over z, x), gy: 4 (over y, core).
Axes of the slice: x: 2, y: 2, z: 4, core: 2. Of those that a mesh axis runs over, the one named last changes fastest.
Arguments:
- dense_grads: float32 [32, 256, 1024], P(('gx', 'gy')), may hold values from -6 to 6
- dense_param: float32 [256, 1024], P(('gx', 'gy')), may hold values from -6 to 6
- dense_acc: float32 [256, 1024], P(('gx', 'gy'))
- table: float32 [131072, 128], P(('gx', 'gy')), may hold values from -6 to 6
- row_acc: float32 [131072], P(('gx', 'gy'))
- touched: int32 [16384], P(('gx', 'gy')), may hold values from 0 to 4095, as said below
- emb_grads: float32 [16384, 128], P(('gx', 'gy'))
Outputs:
- new_dense: float32 [256, 1024], P(('gx', 'gy'))
- new_dense_acc: float32 [256, 1024], P(('gx', 'gy'))
- new_table: float32 [131072, 128], P(('gx', 'gy'))
- new_row_acc: float32 [131072], P(('gx', 'gy'))
Inputs may be any that keep to these rules, and one draw needn't show every extreme that they name: `touched`: within one device's 512 entries no row number repeats.
All inputs are finite; a program needn't handle non-finite values.
Results may differ from a plain program's by a relative error of at most 0.000022.
Values sent between devices are 32-bit elements; how exact they have to be, the bound alone decides.
A program may use at most 128 MiB of HBM per device.

v0:
```python
import jax
import jax.numpy as jnp
from jax import lax
from jax.sharding import PartitionSpec as P

learn_rate = 0.5
max_norm = 8.0
epsilon = 1e-10


def body(dense_grads, dense_param, dense_acc, table, row_acc, touched, emb_grads):
    shards = lax.axis_size(("gx", "gy"))
    local_grad = dense_grads[0]
    embed_square = jnp.sum(emb_grads * emb_grads)
    own_rows = dense_param.shape[0]
    summed, embed_total = lax.psum((local_grad, embed_square), ("gx", "gy"))
    mean_whole = summed / jnp.float32(shards)
    norm_sq = jnp.sum(mean_whole * mean_whole) + embed_total
    start = lax.axis_index(("gx", "gy")) * own_rows
    mean_grad = lax.dynamic_slice_in_dim(mean_whole, start, own_rows, 0)
    clip = jnp.minimum(jnp.float32(1.0), max_norm / (jnp.sqrt(norm_sq) + 1e-06))
    scaled = clip * mean_grad
    new_dense_acc = dense_acc + scaled * scaled
    new_dense = dense_param - learn_rate * scaled / (jnp.sqrt(new_dense_acc) + epsilon)
    row_grads = clip * emb_grads
    square_mean = jnp.mean(row_grads * row_grads, axis=1)
    updated_acc = row_acc[touched] + square_mean
    new_row_acc = row_acc.at[touched].set(updated_acc)
    updated_rows = (
        table[touched] - learn_rate * row_grads / (jnp.sqrt(updated_acc) + epsilon)[:, None]
    )
    new_table = table.at[touched].set(updated_rows)
    return (new_dense, new_dense_acc, new_table, new_row_acc)


def solution(mesh):
    return jax.shard_map(
        body,
        mesh=mesh,
        in_specs=(
            P(("gx", "gy"), None, None),
            P(("gx", "gy"), None),
            P(("gx", "gy"), None),
            P(("gx", "gy"), None),
            P(("gx", "gy")),
            P(("gx", "gy")),
            P(("gx", "gy"), None),
        ),
        out_specs=(
            P(("gx", "gy"), None),
            P(("gx", "gy"), None),
            P(("gx", "gy"), None),
            P(("gx", "gy")),
        ),
        check_vma=False,
    )
```

profile of v0, /device:TPU:0, one launch (start us, length us, event | category | flops | bytes accessed | tf_op | source)
XLA Modules:
  0.0 165.0 jit_solution(8833698111364106730)
XLA Ops:
  7.2 0.0 all-reduce.2.cloned.1.call-start
  7.2 0.7 copy.18
  7.9 0.0 copy-start.3
  7.9 0.0 copy-start.6
  7.9 0.0 all-reduce.2.cloned.1.call-update
  8.0 0.9 copy-done.3
  8.9 0.7 multiply_reduce_fusion.2
  9.5 42.3 %psum.15 = f32[]{:T(128)} all-reduce(f32[]{:T(128)} %multiply_reduce_fusion.2), channel_id=1, replica_groups=mesh['gx'=8,'gy'=4] {'gx','gy'}, use_global_device_ids=true, to_apply=%region_3.0 | all-reduce | flops 1 | bytes 8 | tf_op jit(solution)/shard_map/psum | solution.py:16
  51.9 0.0 copy-done.6
  51.9 3.1 %gather_fusion = f32[512]{0:T(512)S(1)} fusion(f32[4096]{0:T(1024)S(1)} %copy.18, s32[1024]{0:T(1024)S(1)} %pad_clamp_fusion), kind=kCustom, calls=%fused_computation.1 | custom fusion | bytes 6144 | tf_op jit(solution)/shard_map/gather | solution.py:27
  55.0 91.9 %all-reduce.2.cloned.1.call-done = f32[256,1024]{1,0:T(8,128)} async-done(((f32[256,1024]{1,0:T(8,128)}), f32[256,1024]{1,0:T(8,128)}) %all-reduce.2.cloned.1.call-update) | async-done | bytes 1048592 | tf_op jit(solution)/shard_map/psum | solution.py:16
  147.0 2.1 %multiply_reduce_fusion = (f32[]{:T(128)}, f32[256,1024]{1,0:T(8,128)S(1)}) fusion(f32[256,1024]{1,0:T(8,128)} %all-reduce.2.cloned.1.call-done), kind=kLoop, calls=%fused_computation.4 | loop fusion | flops 786431 | bytes 2097156 | tf_op jit(solution)/shard_map/reduce_sum | solution.py:18
  150.5 0.1 multiply_reduce_fusion.1
  150.6 0.0 copy-start.2
  150.6 2.5 %scatter_fusion = f32[4096]{0:T(1024)S(1)} fusion(f32[4096]{0:T(1024)S(1)} %copy.18, s32[512]{0:T(512)S(1)} %compare_select_fusion, f32[512]{0:T(512)S(1)} %get-tuple-element.5), kind=kCustom, calls=%fused_computation.3 | custom fusion | bytes 8192 | tf_op jit(solution)/shard_map/scatter | solution.py:28
  153.1 0.0 copy-start
  153.1 0.0 copy-done.2
  153.1 0.0 copy-start.4
  153.2 0.0 copy-start.5
  153.2 3.6 %scatter_custom_fusion = f32[4096,128]{1,0:T(8,128)S(1)} fusion(f32[4096,128]{1,0:T(8,128)S(1)} %copy-done.2, s32[512]{0:T(512)S(1)} %compare_select_fusion, f32[512,128]{1,0:T(8,128)S(1)} %copy-done.3, f32[512]{0:T(512)S(1)} %get-tuple-element.4, f32[]{:T(128)} %constant.14.clone.1, f32[]{:T(128)S(6)} %min_shard_map.3, s32[1024]{0:T(1024)S(1)} %pad_clamp_fusion), kind=kCustom, calls=%fused_computation.6 | custom fusion | flops 262144 | bytes 4462600 | tf_op jit(solution)/shard_map/scatter | solution.py:32
  156.8 0.0 copy-done
  156.8 0.0 copy-start.1
  156.8 0.0 copy-done.4
  156.8 0.0 copy-done.5
  156.8 0.8 divide_subtract_fusion
  157.6 0.5 copy-done.1
  (3 shorter events, 0.0 us)
Async XLA Ops:
  7.2 139.8 %all-reduce.2.cloned.1.call-start = ((), (), s32[]{:S(2)}) async-start(), calls=%async_computation | async-start | bytes 2097152 | tf_op jit(solution)/shard_map/psum | solution.py:16
  7.9 0.9 copy-start.3
  7.9 43.9 %copy-start.6 = (s32[512]{0:T(512)S(1)}, s32[512]{0:T(512)}, u32[]{:S(2)}) copy-start(s32[512]{0:T(512)} %param.12) | copy-start | bytes 6148
  150.6 2.5 %copy-start.2 = (f32[4096,128]{1,0:T(8,128)S(1)}, f32[4096,128]{1,0:T(8,128)}, u32[]{:S(2)}) copy-start(f32[4096,128]{1,0:T(8,128)} %param.10) | copy-start | bytes 6291460
  153.1 3.7 %copy-start = (f32[4096]{0:T(1024)}, f32[4096]{0:T(1024)S(1)}, u32[]{:S(2)}) copy-start(f32[4096]{0:T(1024)S(1)} %scatter_fusion) | copy-start | bytes 49156
  153.1 3.7 %copy-start.4 = (f32[8,1024]{1,0:T(8,128)S(1)}, f32[8,1024]{1,0:T(8,128)}, u32[]{:S(2)}) copy-start(f32[8,1024]{1,0:T(8,128)} %param.8) | copy-start | bytes 98308
  153.2 3.7 %copy-start.5 = (f32[8,1024]{1,0:T(8,128)S(1)}, f32[8,1024]{1,0:T(8,128)}, u32[]{:S(2)}) copy-start(f32[8,1024]{1,0:T(8,128)} %param.9) | copy-start | bytes 98308
  156.8 1.3 copy-start.1
Sparse Core Ops, SparseCore 0:
  13.2 133.7 all-reduce.1
where the time goes:
time: 165 us
  waiting for transfers between devices  92 us (56%)
  blocking collectives  42.3 us (26%)
  between operations  15.5 us (9%)
  local copies, waits for them, and re-layouts  7.84 us (5%)
  other arithmetic  7.32 us (4%)
    psum x1, waiting for transfers between devices, body(): summed, embed_total = lax.psum((local_grad, embed_square), ('gx', 'gy'))  91.9 us
    psum x1, blocking collectives, body(): summed, embed_total = lax.psum((local_grad, embed_square), ('gx', 'gy'))  42.3 us
    scatter x1, other arithmetic, body(): new_table = table.at[touched].set(updated_rows)  3.6 us
  transfers between devices with their start and end apart: 1, of which 1 were waited for; matrix products, arithmetic and copies ran while one was open for 2% of the time, Pallas kernels for 0%

commit v1 on v0

--- a/solution.py
+++ b/solution.py
@@ -8,12 +8,17 @@
 epsilon = 1e-10
 
 
+def by_each_axis(array, inner_axis, outer_axis):
+    partial = lax.psum(array, inner_axis)
+    return lax.psum(partial, outer_axis)
+
+
 def body(dense_grads, dense_param, dense_acc, table, row_acc, touched, emb_grads):
     shards = lax.axis_size(("gx", "gy"))
     local_grad = dense_grads[0]
     embed_square = jnp.sum(emb_grads * emb_grads)
     own_rows = dense_param.shape[0]
-    summed, embed_total = lax.psum((local_grad, embed_square), ("gx", "gy"))
+    summed, embed_total = by_each_axis((local_grad, embed_square), "gy", "gx")
     mean_whole = summed / jnp.float32(shards)
     norm_sq = jnp.sum(mean_whole * mean_whole) + embed_total
     start = lax.axis_index(("gx", "gy")) * own_rows

time: 165 us -> 150 us (0.909)
  blocking collectives: 42.3 us -> 28.8 us
    psum x1 -> x2, blocking collectives: 42.3 us -> 28.8 us  [the longest x1 22.3 us: by_each_axis(): return lax.psum(partial, outer_axis)]
    psum x1 -> x2, waiting for transfers between devices: 91.9 us -> 91 us  [the longest x1 49.6 us: by_each_axis(): return lax.psum(partial, outer_axis)]
  transfers between devices with their start and end apart: 1 -> 2, of which waited for: 1 -> 2; matrix products, arithmetic and copies ran while one was open for 2% -> 3% of each run, Pallas kernels for 0% -> 0%
where the time goes in v1:
time: 150 us
  waiting for transfers between devices  91 us (61%)
  blocking collectives  28.8 us (19%)
  between operations  15.5 us (10%)
  other arithmetic  7.31 us (5%)
  local copies, waits for them, and re-layouts  6.93 us (5%)
    psum x1, waiting for transfers between devices, by_each_axis(): return lax.psum(partial, outer_axis)  49.6 us
    psum x1, waiting for transfers between devices, by_each_axis(): partial = lax.psum(array, inner_axis)  41.4 us
    psum x1, blocking collectives, by_each_axis(): return lax.psum(partial, outer_axis)  22.3 us
    psum x1, blocking collectives, by_each_axis(): partial = lax.psum(array, inner_axis)  6.52 us
    scatter x1, other arithmetic, body(): new_table = table.at[touched].set(updated_rows)  3.6 us
    gather x1, local copies, waits for them, and re-layouts, body(): updated_acc = row_acc[touched] + square_mean  3.14 us
  transfers between devices with their start and end apart: 2, of which 2 were waited for; matrix products, arithmetic and copies ran while one was open for 3% of the time, Pallas kernels for 0%

profile of v1, /device:TPU:0, one launch (start us, length us, event | category | flops | bytes accessed | tf_op | source)
XLA Modules:
  0.0 149.7 jit_solution(11305364697682878015)
XLA Ops:
  7.2 0.0 all-reduce.3.cloned.1.call-start
  7.2 0.7 copy.19
  7.9 0.0 copy-start.3
  7.9 0.0 copy-start.6
  7.9 0.0 all-reduce.3.cloned.1.call-update
  8.0 0.0 all-reduce.5.cloned.1.call-start
  8.0 41.4 %all-reduce.3.cloned.1.call-done = f32[256,1024]{1,0:T(8,128)} async-done(((f32[256,1024]{1,0:T(8,128)}), f32[256,1024]{1,0:T(8,128)}) %all-reduce.3.cloned.1.call-update) | async-done | bytes 1048592 | tf_op jit(solution)/shard_map/psum | solution.py:12
  49.4 0.0 all-reduce.5.cloned.1.call-update
  49.4 0.0 copy-done.3
  49.4 0.7 multiply_reduce_fusion.2
  50.1 6.5 %psum.30 = f32[]{:T(128)} all-reduce(f32[]{:T(128)} %multiply_reduce_fusion.2), channel_id=1, replica_groups=mesh['gx'=8,'gy'=4] {'gy'}, use_global_device_ids=true, to_apply=%region_4.0 | all-reduce | flops 1 | bytes 8 | tf_op jit(solution)/shard_map/psum | solution.py:12
  56.6 22.3 %psum.31 = f32[]{:T(128)} all-reduce(f32[]{:T(128)} %psum.30), channel_id=1, replica_groups=mesh['gx'=8,'gy'=4] {'gx'}, use_global_device_ids=true, to_apply=%region_5.0 | all-reduce | flops 1 | bytes 8 | tf_op jit(solution)/shard_map/psum | solution.py:13
  78.9 0.0 copy-done.6
  78.9 3.1 %gather_fusion = f32[512]{0:T(512)S(1)} fusion(f32[4096]{0:T(1024)S(1)} %copy.19, s32[1024]{0:T(1024)S(1)} %pad_clamp_fusion), kind=kCustom, calls=%fused_computation.1 | custom fusion | bytes 6144 | tf_op jit(solution)/shard_map/gather | solution.py:32
  82.1 49.6 %all-reduce.5.cloned.1.call-done = f32[256,1024]{1,0:T(8,128)} async-done(((f32[256,1024]{1,0:T(8,128)}), f32[256,1024]{1,0:T(8,128)}) %all-reduce.5.cloned.1.call-update) | async-done | bytes 1048592 | tf_op jit(solution)/shard_map/psum | solution.py:13
  131.7 2.1 %multiply_reduce_fusion = (f32[]{:T(128)}, f32[256,1024]{1,0:T(8,128)S(1)}) fusion(f32[256,1024]{1,0:T(8,128)} %all-reduce.5.cloned.1.call-done), kind=kLoop, calls=%fused_computation.4 | loop fusion | flops 786431 | bytes 2097156 | tf_op jit(solution)/shard_map/reduce_sum | solution.py:23
  135.2 0.1 multiply_reduce_fusion.1
  135.4 0.0 copy-start.2
  135.4 2.5 %scatter_fusion = f32[4096]{0:T(1024)S(1)} fusion(f32[4096]{0:T(1024)S(1)} %copy.19, s32[512]{0:T(512)S(1)} %compare_select_fusion, f32[512]{0:T(512)S(1)} %get-tuple-element.5), kind=kCustom, calls=%fused_computation.3 | custom fusion | bytes 8192 | tf_op jit(solution)/shard_map/scatter | solution.py:33
  137.9 0.0 copy-start
  137.9 0.0 copy-done.2
  137.9 0.0 copy-start.4
  137.9 0.0 copy-start.5
  137.9 3.6 %scatter_custom_fusion = f32[4096,128]{1,0:T(8,128)S(1)} fusion(f32[4096,128]{1,0:T(8,128)S(1)} %copy-done.2, s32[512]{0:T(512)S(1)} %compare_select_fusion, f32[512,128]{1,0:T(8,128)S(1)} %copy-done.3, f32[512]{0:T(512)S(1)} %get-tuple-element.4, f32[]{:T(128)} %constant.14.clone.1, f32[]{:T(128)S(6)} %min_shard_map.3, s32[1024]{0:T(1024)S(1)} %pad_clamp_fusion), kind=kCustom, calls=%fused_computation.6 | custom fusion | flops 262144 | bytes 4462600 | tf_op jit(solution)/shard_map/scatter | solution.py:37
  141.5 0.0 copy-done
  141.5 0.0 copy-start.1
  141.5 0.0 copy-done.4
  141.6 0.0 copy-done.5
  141.6 0.8 divide_subtract_fusion
  142.3 0.5 copy-done.1
  (3 shorter events, 0.0 us)
Async XLA Ops:
  7.2 42.2 %all-reduce.3.cloned.1.call-start = ((), (), s32[]{:S(2)}) async-start(), calls=%async_computation | async-start | bytes 2097152 | tf_op jit(solution)/shard_map/psum | solution.py:12
  7.9 41.5 %copy-start.3 = (f32[512,128]{1,0:T(8,128)S(1)}, f32[512,128]{1,0:T(8,128)}, u32[]{:S(2)}) copy-start(f32[512,128]{1,0:T(8,128)} %param.13) | copy-start | bytes 786436
  7.9 71.0 %copy-start.6 = (s32[512]{0:T(512)S(1)}, s32[512]{0:T(512)}, u32[]{:S(2)}) copy-start(s32[512]{0:T(512)} %param.12) | copy-start | bytes 6148
  8.0 123.7 %all-reduce.5.cloned.1.call-start = ((), (), s32[]{:S(2)}) async-start(), calls=%async_computation.1 | async-start | bytes 2097152 | tf_op jit(solution)/shard_map/psum | solution.py:13
  135.4 2.5 %copy-start.2 = (f32[4096,128]{1,0:T(8,128)S(1)}, f32[4096,128]{1,0:T(8,128)}, u32[]{:S(2)}) copy-start(f32[4096,128]{1,0:T(8,128)} %param.10) | copy-start | bytes 6291460
  137.9 3.7 %copy-start = (f32[4096]{0:T(1024)}, f32[4096]{0:T(1024)S(1)}, u32[]{:S(2)}) copy-start(f32[4096]{0:T(1024)S(1)} %scatter_fusion) | copy-start | bytes 49156
  137.9 3.7 %copy-start.4 = (f32[8,1024]{1,0:T(8,128)S(1)}, f32[8,1024]{1,0:T(8,128)}, u32[]{:S(2)}) copy-start(f32[8,1024]{1,0:T(8,128)} %param.8) | copy-start | bytes 98308
  137.9 3.7 %copy-start.5 = (f32[8,1024]{1,0:T(8,128)S(1)}, f32[8,1024]{1,0:T(8,128)}, u32[]{:S(2)}) copy-start(f32[8,1024]{1,0:T(8,128)} %param.9) | copy-start | bytes 98308
  141.5 1.3 copy-start.1
Sparse Core Ops, SparseCore 0:
  10.3 38.9 all-reduce.2
  52.9 78.7 all-reduce.4
